TPU v7x, 32 devices: a whole 2x2x4 slice. The times are simulated.
32 devices in a mesh: lat: 4 (over z), lon: 8 (over y, x, core).
Axes of the slice: x: 2, y: 2, z: 4, core: 2. Of those that a mesh axis runs over, the one named last changes fastest.
Arguments:
- surface_forcing: float32 [4320, 1024], P('lon', 'lat'), may hold values from -40 to 40
- ocean_mask: int32 [4320, 1024], P('lon', 'lat'), may hold values 0 or 1
- self_coupling: float32 [4320, 1024], P('lon', 'lat'), may hold values from 0.2 to 2
- east_coupling: float32 [4320, 1024], P('lon', 'lat'), may hold values from 0.3 to 3
- north_coupling: float32 [4320, 1024], P('lon', 'lat'), may hold values from 0.3 to 3
- zonal_weight: float32 [1024], P('lat'), may hold values from 0.5 to 50
- aligned_inverse: float32 [8, 128, 128], P('lat'), may hold values from -1 to 4, as said below
- staggered_inverse: float32 [8, 128, 128], P('lat'), may hold values from -1 to 4, as said below
Outputs:
- solution: float32 [4320, 1024], P('lon', 'lat')
- residual: float32 [4320, 1024], P('lon', 'lat')
- direction: float32 [4320, 1024], P('lon', 'lat')
Inputs may be any that keep to these rules, and one draw needn't show every extreme that they name: `aligned_inverse`: each block is symmetric and positive definite. `staggered_inverse`: each block is symmetric and positive definite.
All inputs are finite; a program needn't handle non-finite values. No bound on the sum of `ocean_mask` on one device may be relied on, other than what follows from the above.
Results may differ from a plain program's by a relative error of at most 0.00023.
Values sent between devices are 32-bit elements; how exact they have to be, the bound alone decides.
A program may use at most 64 MiB of HBM per device.

v0:
```python
import functools

import jax
import jax.numpy as jnp
import numpy as np
from jax import lax
from jax.experimental import pallas as pl
from jax.experimental.pallas import tpu as pltpu
from jax.sharding import PartitionSpec as P

MESH = pl.DeviceIdType.MESH


def outer_table(groups):
    table = np.zeros((groups, groups))
    place = np.arange(groups)
    table[0] = 1.0
    table[1] = np.where(place % 2 == 0, 1.0, -1.0)
    for mode in range(1, groups // 2):
        turn = 2.0 * np.pi * (mode * place % groups) / groups
        table[2 * mode] = np.cos(turn)
        table[2 * mode + 1] = -np.sin(turn)
    table[np.abs(table) < 1e-12] = 0.0
    return table


def inner_tables(groups, length, padded):
    total = groups * length
    pairs = groups // 2
    matrix = np.zeros((pairs, 2 * padded, 2 * padded))
    waves = np.zeros((pairs, 2 * padded))
    weights = np.zeros((pairs, 2 * padded))
    cell = np.arange(length)

    def turns(modes):
        return 2.0 * np.pi * (modes[:, None] * cell[None, :] % total) / total

    def note(pair, start, modes):
        stop = start + len(modes)
        waves[pair, start:stop] = 2.0 - 2.0 * np.cos(2.0 * np.pi * modes / total)
        weights[pair, start:stop] = np.where(modes * 2 % total == 0, 1.0, 2.0) / total

    for part, (first, real_count) in enumerate(((0, length // 2 + 1), (groups // 2, (length + 1) // 2))):
        skipped = 1 if part == 0 else 0
        real = first + groups * np.arange(real_count)
        imag = first + groups * (skipped + np.arange(length - real_count))
        row = part * padded
        columns = slice(part * padded, part * padded + length)
        matrix[0, row : row + real_count, columns] = np.cos(turns(real))
        matrix[0, row + real_count : row + length, columns] = -np.sin(turns(imag))
        note(0, row, real)
        note(0, row + real_count, imag)
    for pair in range(1, pairs):
        modes = pair + groups * np.arange(length)
        angle = turns(modes)
        low, high = slice(0, length), slice(padded, padded + length)
        matrix[pair, low, low] = np.cos(angle)
        matrix[pair, low, high] = np.sin(angle)
        matrix[pair, high, low] = -np.sin(angle)
        matrix[pair, high, high] = np.cos(angle)
        note(pair, 0, modes)
        note(pair, padded, modes)
    single = matrix.astype(np.float32)
    leading = single.astype(jnp.bfloat16)
    rest = (matrix - leading.astype(np.float64)).astype(jnp.bfloat16)
    return np.stack([leading, rest], axis=1), waves.astype(np.float32), weights.astype(np.float32)


def parted(value):
    leading = value.astype(jnp.bfloat16)
    return leading, (value - leading.astype(jnp.float32)).astype(jnp.bfloat16)


def product(left, right):
    dot = functools.partial(jnp.dot, preferred_element_type=jnp.float32)
    return dot(left[0], right[0]) + (dot(left[0], right[1]) + dot(left[1], right[0]))


def weighted(values, factors):
    total = None
    for value, factor in zip(values, factors):
        if factor == 0.0:
            continue
        term = value if factor == 1.0 else value * np.float32(factor)
        total = term if total is None else total + term
    return total


def kernel(
    groups, bands, chunk, block, tile, table,
    x_ref, matrix_ref, merid_ref, scale_ref, scale_out_ref, out_ref,
    got1, send2, got2, halo_out, halo_in, spectrum, send3, got3, send4, got4, matrix,
    load_sem, send_sem, recv_sem, halo_send, halo_recv,
):
    band = lax.axis_index("lat")
    me = lax.axis_index("lon")
    pair, core = me // 2, me % 2
    padded = groups * chunk
    half = block // 2
    mate = me + 1 - 2 * core
    across = band - 1 + 2 * core
    has_across = (across >= 0) & (across < bands)

    load = pltpu.make_async_copy(matrix_ref.at[pair], matrix, load_sem)
    load.start()
    barrier = pltpu.get_barrier_semaphore()
    for step in range(1, groups):
        pl.semaphore_signal(
            barrier, inc=1, device_id=(band, (me + step) % groups), device_id_type=MESH
        )

    @pl.when(has_across)
    def _():
        pl.semaphore_signal(barrier, inc=1, device_id=(across, mate), device_id_type=MESH)

    pl.semaphore_wait(barrier, groups - 1 + has_across.astype(jnp.int32))

    def rows(index):
        return pl.ds(pl.multiple_of(index * chunk, 8), chunk)

    def exchange(phase, source, target):
        def copies(step, to, slot):
            return [
                pltpu.make_async_remote_copy(
                    src_ref=piece,
                    dst_ref=place,
                    send_sem=send_sem.at[phase, step, part],
                    recv_sem=recv_sem.at[phase, step, part],
                    device_id=(band, to),
                    device_id_type=MESH,
                )
                for part, (piece, place) in enumerate(zip(source(to), target(slot)))
            ]

        started = []
        for step in range(1, groups):
            started.append(copies(step, (me + step) % groups, me))
            for copy in started[-1]:
                copy.start()

        def finish():
            for step in range(1, groups):
                origin = (me - step + groups) % groups
                for copy in copies(step, origin, origin):
                    copy.wait_recv()

        def drain():
            for batch in started:
                for copy in batch:
                    copy.wait_send()

        return finish, drain

    finish1, drain1 = exchange(0, lambda to: [x_ref.at[rows(to)]], lambda slot: [got1.at[slot]])
    got1[me] = x_ref[rows(me), :]
    finish1()
    for side in range(2):
        lanes = slice(side * block, (side + 1) * block)
        values = [got1[place, :, lanes] for place in range(groups)]
        for row in range(groups):
            send2[row // 2, side, row % 2] = weighted(values, table[row])
    finish2, drain2 = exchange(
        1,
        lambda to: [send2.at[to // 2, to % 2]],
        lambda slot: [got2.at[:, rows(slot), :]],
    )
    got2[:, rows(me), :] = send2[pair, core]
    load.wait()
    finish2()

    cells = parted(got2[...].reshape(2 * padded, block))

    def forward(index, carry):
        span = pl.ds(pl.multiple_of(index * tile, 128), tile)
        spectrum[span, :] = (
            product((matrix[0, span, :], matrix[1, span, :]), cells) * scale_ref[span, :]
        )
        return carry

    lax.fori_loop(0, 2 * padded // tile, forward, 0)

    upper, lower = spectrum[:padded, :], spectrum[padded:, :]
    left = lax.broadcasted_iota(jnp.int32, (padded, block), 1) < half
    halo_out[0] = jnp.where(left, pltpu.roll(upper, half, 1), lower)
    halo_out[1] = jnp.where(left, upper, pltpu.roll(lower, half, 1))

    def halo(slot, to_band):
        return pltpu.make_async_remote_copy(
            src_ref=halo_out.at[slot],
            dst_ref=halo_in.at[slot],
            send_sem=halo_send.at[slot],
            recv_sem=halo_recv.at[slot],
            device_id=(to_band, mate),
            device_id_type=MESH,
        )

    go_up = (core == 0) | (band < bands - 1)
    go_down = (core == 1) | (band > 0)
    up, down = halo(0, band + core), halo(1, band - 1 + core)

    @pl.when(go_up)
    def _():
        up.start()

    @pl.when(go_down)
    def _():
        down.start()

    @pl.when(jnp.logical_not(go_down))
    def _():
        halo_in[0] = jnp.zeros((padded, block), jnp.float32)

    @pl.when(jnp.logical_not(go_up))
    def _():
        halo_in[1] = jnp.zeros((padded, block), jnp.float32)

    own = product(parted(spectrum[...]), parted(merid_ref[:block, :]))

    @pl.when(go_down)
    def _():
        halo(0, band - 1 + core).wait_recv()

    @pl.when(go_up)
    def _():
        halo(1, band + core).wait_recv()

    below, above = halo_in[0], halo_in[1]
    beside = jnp.concatenate(
        [
            jnp.where(left, below, pltpu.roll(above, half, 1)),
            jnp.where(left, pltpu.roll(below, half, 1), above),
        ],
        axis=0,
    )
    mixed = own + product(parted(beside), parted(merid_ref[block:, :]))
    turned = parted((mixed * scale_out_ref[...]).T)

    def backward(index, carry):
        span = pl.ds(pl.multiple_of(index * tile, 128), tile)
        send3[span, :] = product(turned, (matrix[0, :, span], matrix[1, :, span])).T
        return carry

    lax.fori_loop(0, 2 * padded // tile, backward, 0)

    def portions(to):
        return [
            send3.at[pl.ds(pl.multiple_of(part * padded + to * chunk, 8), chunk)]
            for part in range(2)
        ]

    finish3, drain3 = exchange(2, portions, lambda slot: [got3.at[slot, 0], got3.at[slot, 1]])
    for part in range(2):
        got3[me, part] = send3[pl.ds(pl.multiple_of(part * padded + me * chunk, 8), chunk), :]
    finish3()
    for side in range(2):
        lanes = slice(side * block, (side + 1) * block)
        values = [got3[2 * (row // 2) + side, row % 2] for row in range(groups)]
        for place in range(groups):
            send4[place, :, lanes] = weighted(values, table[:, place])
    finish4, drain4 = exchange(3, lambda to: [send4.at[to]], lambda slot: [got4.at[rows(slot)]])
    got4[rows(me), :] = send4[me]
    finish4()
    out_ref[...] = got4[...]
    for drain in (drain1, drain2, drain3, drain4):
        drain()

    @pl.when(go_up)
    def _():
        up.wait_send()

    @pl.when(go_down)
    def _():
        down.wait_send()


def local(
    surface_forcing,
    ocean_mask,
    self_coupling,
    east_coupling,
    north_coupling,
    zonal_weight,
    aligned_inverse,
    staggered_inverse,
):
    groups, bands = lax.axis_size("lon"), lax.axis_size("lat")
    band, me = lax.axis_index("lat"), lax.axis_index("lon")
    length, columns = surface_forcing.shape
    block = aligned_inverse.shape[1]
    half = block // 2
    assert columns == 2 * block and groups % 2 == 0
    chunk = -(-length // (8 * groups)) * 8
    padded = groups * chunk
    while 2 * padded % 128:
        chunk, padded = chunk + 8, padded + 8 * groups
    width = 2 * padded
    tile = next(t for t in (384, 256, 128) if width % t == 0)
    table = outer_table(groups)
    matrix, waves, weights = inner_tables(groups, length, padded)
    pair, core = me // 2, me % 2

    wave = lax.dynamic_index_in_dim(jnp.asarray(waves), pair, 0, False)
    weight = lax.dynamic_index_in_dim(jnp.asarray(weights), pair, 0, False)
    zonal = lax.dynamic_slice_in_dim(zonal_weight, core * block, block)
    scale = lax.rsqrt(1.0 + wave[:, None] * zonal[None, :])
    scale_out = scale * weight[:, None]

    count = aligned_inverse.shape[0]
    carried = lax.ppermute(
        staggered_inverse[count - 1], "lat", [(i, i + 1) for i in range(bands - 1)]
    )
    aligned = lax.dynamic_index_in_dim(aligned_inverse, core, 0, False)
    above = lax.dynamic_index_in_dim(staggered_inverse, core, 0, False)
    below = jnp.where(core == 0, carried, staggered_inverse[0])
    zero = jnp.zeros((half, half), jnp.float32)
    inside = aligned + jnp.block([[below[half:, half:], zero], [zero, above[:half, :half]]])
    beside = jnp.block([[below[half:, :half], zero], [zero, above[:half, half:]]])
    merid = jnp.concatenate([inside, beside], axis=1).T

    f32 = jnp.float32
    vmem = pl.BlockSpec(memory_space=pltpu.VMEM)
    call = pl.pallas_call(
        functools.partial(kernel, groups, bands, chunk, block, tile, table),
        out_shape=jax.ShapeDtypeStruct((padded, columns), f32),
        in_specs=[vmem, pl.BlockSpec(memory_space=pl.ANY), vmem, vmem, vmem],
        out_specs=vmem,
        scratch_shapes=[
            pltpu.VMEM((groups, chunk, columns), f32),
            pltpu.VMEM((groups // 2, 2, 2, chunk, block), f32),
            pltpu.VMEM((2, padded, block), f32),
            pltpu.VMEM((2, padded, block), f32),
            pltpu.VMEM((2, padded, block), f32),
            pltpu.VMEM((width, block), f32),
            pltpu.VMEM((width, block), f32),
            pltpu.VMEM((groups, 2, chunk, block), f32),
            pltpu.VMEM((groups, chunk, columns), f32),
            pltpu.VMEM((padded, columns), f32),
            pltpu.VMEM((2, width, width), jnp.bfloat16),
            pltpu.SemaphoreType.DMA,
            pltpu.SemaphoreType.DMA((4, groups, 2)),
            pltpu.SemaphoreType.DMA((4, groups, 2)),
            pltpu.SemaphoreType.DMA((2,)),
            pltpu.SemaphoreType.DMA((2,)),
        ],
        compiler_params=pltpu.CompilerParams(
            collective_id=0, has_side_effects=True, vmem_limit_bytes=40 * 2**20
        ),
        cost_estimate=pl.CostEstimate(
            flops=40_000 * width * block, bytes_accessed=8 * width * width, transcendentals=0
        ),
        name="zonal_precondition",
    )
    constants = jnp.asarray(matrix)

    def precondition(field):
        grown = jnp.pad(field, ((0, padded - length), (0, 0)))
        return call(grown, constants, merid, scale, scale_out)[:length]

    ring = [(i, (i + 1) % groups) for i in range(groups)]
    back_ring = [(b, a) for a, b in ring]
    line = [(i, i + 1) for i in range(bands - 1)]
    back_line = [(b, a) for a, b in line]

    wet = ocean_mask.astype(f32)
    east_wet = east_coupling * wet
    north_wet = north_coupling * wet
    wet_east = jnp.concatenate([wet[1:], lax.ppermute(wet[:1], "lon", back_ring)], axis=0)
    wet_north = jnp.concatenate([wet[:, 1:], lax.ppermute(wet[:, :1], "lat", back_line)], axis=1)
    east_west = jnp.concatenate([lax.ppermute(east_wet[-1:], "lon", ring), east_wet[:-1]], axis=0)
    north_south = jnp.concatenate(
        [lax.ppermute(north_wet[:, -1:], "lat", line), north_wet[:, :-1]], axis=1
    )
    east = east_wet * wet_east
    north = north_wet * wet_north
    west = east_west * wet
    south = north_south * wet

    rhs_wet = wet * surface_forcing
    first = wet * precondition(rhs_wet)
    from_east = lax.ppermute(first[:1], "lon", back_ring)
    from_west = lax.ppermute(first[-1:], "lon", ring)
    from_north = lax.ppermute(first[:, :1], "lat", back_line)
    from_south = lax.ppermute(first[:, -1:], "lat", line)
    image = (1.0 - wet) * first + wet * self_coupling * first
    image = image + east * (first - jnp.concatenate([first[1:], from_east], axis=0))
    image = image + west * (first - jnp.concatenate([from_west, first[:-1]], axis=0))
    image = image + north * (first - jnp.concatenate([first[:, 1:], from_north], axis=1))
    image = image + south * (first - jnp.concatenate([from_south, first[:, :-1]], axis=1))
    sums = lax.psum(
        jnp.stack([jnp.sum(rhs_wet * first), jnp.sum(first * image)]), ("lat", "lon")
    )
    rz_now = sums[0]
    alpha = rz_now / sums[1]
    filtered = wet * precondition(image)
    solved = alpha * first
    residual = rhs_wet - alpha * image
    second = first - alpha * filtered
    rz_next = lax.psum(jnp.sum(residual * second), ("lat", "lon"))
    direction = second + rz_next / rz_now * first
    return (solved, residual, direction)


def solution(mesh):
    grid = P("lon", "lat")
    stack = P("lat", None, None)
    return jax.shard_map(
        local,
        mesh=mesh,
        in_specs=(grid, grid, grid, grid, grid, P("lat"), stack, stack),
        out_specs=(grid, grid, grid),
        check_vma=False,
    )
```

profile of v0, /device:TPU:0, one launch (start us, length us, event | category | flops | bytes accessed | tf_op | source)
XLA Modules:
  0.0 225.5 jit_solution(8382673134250047856)
XLA Ops:
  0.6 0.0 copy-start
  0.6 0.0 copy-start.1
  0.7 1.0 fusion.18
  1.7 0.1 copy.18
  1.8 5.0 %collective-permute-start = (f32[128,128]{0,1:T(8,128)S(1)}, f32[128,128]{0,1:T(8,128)S(1)}, u32[]{:S(2)}, u32[]{:S(2)}) collective-permute-start(f32[128,128]{0,1:T(8,128)S(1)} %bitcast.17), channel_id=1, source_target_pairs={{0,8},{8,16},{16,24},{1,9},{9,17},{17,25},{2,10},{10,18},{18,26},{... | collective-permute-start | bytes 196616 | tf_op jit(solution)/shard_map/ppermute | solution.py:309
  6.7 1.1 convert_element_type.6
  7.8 0.6 slice.109
  8.4 1.6 collective-permute-start.1
  10.0 0.7 slice.117
  10.7 1.3 collective-permute-start.5
  12.0 1.7 convert_multiply_fusion.1
  13.8 0.0 copy-start.3
  13.8 0.0 copy-start.5
  13.8 0.0 copy-start.2
  13.8 0.7 slice.112
  14.4 0.0 collective-permute-start.3
  14.4 0.8 slice.120
  15.3 5.3 %collective-permute-start.7 = (f32[540,1]{1,0:T(8,128)}, f32[540,1]{1,0:T(8,128)}, u32[]{:S(2)}, u32[]{:S(2)}) collective-permute-start(f32[540,1]{1,0:T(8,128)} %slice.120), channel_id=1, source_target_pairs={{0,8},{8,16},{16,24},{1,9},{9,17},{17,25},{2,10},{10,18},{18,26},{... | collective-permute-start | bytes 6488 | tf_op jit(solution)/shard_map/ppermute | solution.py:371
  20.6 0.8 slice.108
  21.4 1.0 slice.116
  22.4 0.1 copy.17
  22.5 0.8 dynamic_slice.20
  23.3 0.8 dynamic-slice_reduce_fusion
  24.1 0.0 copy-done.3
  24.1 0.0 copy-done.5
  24.1 0.4 broadcast_multiply_fusion
  24.5 0.0 copy-done
  24.5 0.1 copy.14
  24.6 0.1 copy.19
  24.7 0.0 copy-start.4
  24.7 0.0 copy-start.6
  24.7 0.0 copy-start.7
  24.7 0.0 copy-start.8
  24.8 0.0 collective-permute-done
  24.8 0.1 fusion.19
  24.9 0.1 fusion.12
  25.0 0.1 fusion.9.merid_ref
  25.1 43.2 %zonal_precondition.2 = f32[576,256]{1,0:T(8,128)S(1)} custom-call(f32[576,256]{1,0:T(8,128)S(1)} %pad.11.x_ref, bf16[4,2,1152,1152]{3,2,1,0:T(8,128)(2,1)} %constant.61.clone.matrix_ref, f32[256,128]{1,0:T(8,128)S(1)} %fusion.9.merid_ref, f32[1152,128]{1,0:T(8,128)S(1)} %get-tuple-element.29.scale_ref, f32[1152,128]{1,0:T(8,128)S(1)} %get-tuple-element.28.scale_out_ref), custom_call_target="tpu_custom_call" | custom-call | flops 5898240000 | bytes 10616832 | tf_op jit(solution)/shard_map/zonal_precondition/pallas_call | solution.py:357
  68.3 0.1 slice_multiply_fusion
  68.4 0.1 fusion.17
  68.5 0.2 fusion.16
  68.8 2.4 %collective-permute-start.2 = (f32[1,256]{1,0:T(1,128)S(1)}, f32[1,256]{1,0:T(1,128)S(1)}, u32[]{:S(2)}, u32[]{:S(2)}) collective-permute-start(f32[1,256]{1,0:T(1,128)S(1)} %get-tuple-element.12), channel_id=1, source_target_pairs={{1,0},{2,1},{3,2},{4,3},{5,4},{6,5},{7,6},{0,7},{9,8},{10,9},{11,1... | collective-permute-start | bytes 3080 | tf_op jit(solution)/shard_map/ppermute | solution.py:380
  71.2 0.0 collective-permute-done.1
  71.2 0.0 collective-permute-start.4
  71.2 0.0 collective-permute-done.3
  71.2 1.3 collective-permute-start.6
  72.5 0.0 collective-permute-done.5
  72.5 6.8 %collective-permute-start.8 = (f32[540,1]{1,0:T(8,128)S(1)}, f32[540,1]{1,0:T(8,128)S(1)}, u32[]{:S(2)}, u32[]{:S(2)}) collective-permute-start(f32[540,1]{1,0:T(8,128)S(1)} %get-tuple-element.20), channel_id=1, source_target_pairs={{0,8},{8,16},{16,24},{1,9},{9,17},{17,25},{2,10},{10,18},{18,26},{... | collective-permute-start | bytes 6488 | tf_op jit(solution)/shard_map/ppermute | solution.py:383
  79.3 0.1 fusion.14
  79.4 0.0 collective-permute-done.7
  79.4 0.0 collective-permute-done.2
  79.4 0.0 collective-permute-done.4
  79.4 5.4 %collective-permute-done.6 = f32[540,1]{1,0:T(8,128)S(1)} collective-permute-done((f32[540,1]{1,0:T(8,128)S(1)}, f32[540,1]{1,0:T(8,128)S(1)}, u32[]{:S(2)}, u32[]{:S(2)}) %collective-permute-start.6) | collective-permute-done | bytes 2192 | tf_op jit(solution)/shard_map/ppermute | solution.py:382
  84.8 1.2 collective-permute-done.8
  86.0 0.0 copy-done.8
  86.0 3.8 %multiply_reduce_fusion.2 = (f32[]{:T(128)}, f32[]{:T(128)}, f32[540,256]{1,0:T(8,128)}) fusion(f32[540,256]{1,0:T(8,128)S(1)} %get-tuple-element.15, f32[540,256]{1,0:T(8,128)S(1)} %slice_multiply_fusion, f32[540,255]{1,0:T(8,128)S(1)} %get-tuple-element.18, f32[540,1]{1,0:T(8,128)S(1)} %collective-permute-done.8, f32[540,255]{1,0:T(8,128)S(1)} %bitcast.14, ...), kind=kLoop, calls=%fused_computation.22 | loop fusion | flops 4838398 | bytes 8294408 | tf_op jit(solution)/shard_map/reduce_sum | solution.py:390
  89.8 1.4 pad_maximum_fusion
  91.2 40.5 %psum.14 = f32[2]{0:T(128)S(1)} all-reduce(f32[2]{0:T(128)S(1)} %pad_maximum_fusion), channel_id=1, replica_groups=mesh['lat'=4,'lon'=8] {'lat','lon'}, use_global_device_ids=true, to_apply=%region_2.3 | all-reduce | flops 2 | bytes 16 | tf_op jit(solution)/shard_map/psum | solution.py:389
  131.6 0.6 fusion.21
  132.2 1.1 pad.12.x_ref
  133.3 43.4 %zonal_precondition.3 = f32[576,256]{1,0:T(8,128)S(1)} custom-call(f32[576,256]{1,0:T(8,128)S(1)} %pad.12.x_ref, bf16[4,2,1152,1152]{3,2,1,0:T(8,128)(2,1)} %constant.61.clone.matrix_ref, f32[256,128]{1,0:T(8,128)S(1)} %fusion.9.merid_ref, f32[1152,128]{1,0:T(8,128)S(1)} %get-tuple-element.29.scale_ref, f32[1152,128]{1,0:T(8,128)S(1)} %get-tuple-element.28.scale_out_ref), custom_call_target="tpu_custom_call" | custom-call | flops 5898240000 | bytes 10616832 | tf_op jit(solution)/shard_map/zonal_precondition/pallas_call | solution.py:357
  178.1 2.8 %multiply_reduce_fusion = (f32[]{:T(128)}, f32[540,256]{1,0:T(8,128)}) fusion(f32[540,256]{1,0:T(8,128)S(1)} %slice_multiply_fusion, f32[576,256]{1,0:T(8,128)S(1)} %zonal_precondition.3, f32[]{:T(128)S(6)} %div.17, s32[540,256]{1,0:T(8,128)S(1)} %copy-done.1, f32[540,256]{1,0:T(8,128)} %copy-done.2, f32[540,256]{1,0:T(8,128)} %get-tuple-element.7), kind=kLoop, calls=%fused_computation.18 | loop fusion | flops 1105919 | bytes 3317768 | tf_op jit(solution)/shard_map/reduce_sum | solution.py:398
  180.9 42.1 %psum.15 = f32[]{:T(128)} all-reduce(f32[]{:T(128)} %get-tuple-element.5), channel_id=1, replica_groups=mesh['lat'=4,'lon'=8] {'lat','lon'}, use_global_device_ids=true, to_apply=%region_4.5 | all-reduce | flops 1 | bytes 8 | tf_op jit(solution)/shard_map/psum | solution.py:398
  224.4 1.1 multiply_add_fusion
  (10 shorter events, 0.1 us)
Async XLA Ops:
  0.6 23.8 %copy-start = (f32[2,128,128]{2,1,0:T(8,128)S(1)}, f32[2,128,128]{2,1,0:T(8,128)}, u32[]{:S(2)}) copy-start(f32[2,128,128]{2,1,0:T(8,128)} %param.17) | copy-start | bytes 393220
  0.6 67.7 %copy-start.1 = (s32[540,256]{1,0:T(8,128)S(1)}, s32[540,256]{1,0:T(8,128)}, u32[]{:S(2)}) copy-start(s32[540,256]{1,0:T(8,128)} %param.12) | copy-start | bytes 1658884
  1.8 23.0 %collective-permute-start = (f32[128,128]{0,1:T(8,128)S(1)}, f32[128,128]{0,1:T(8,128)S(1)}, u32[]{:S(2)}, u32[]{:S(2)}) collective-permute-start(f32[128,128]{0,1:T(8,128)S(1)} %bitcast.17), channel_id=1, source_target_pairs={{0,8},{8,16},{16,24},{1,9},{9,17},{17,25},{2,10},{10,18},{18,26},{... | collective-permute-start | bytes 196616 | tf_op jit(solution)/shard_map/ppermute | solution.py:309
  8.4 62.8 %collective-permute-start.1 = (f32[1,256]{1,0:T(1,128)}, f32[1,256]{1,0:T(1,128)}, u32[]{:S(2)}, u32[]{:S(2)}) collective-permute-start(f32[1,256]{1,0:T(1,128)} %slice.109), channel_id=1, source_target_pairs={{1,0},{2,1},{3,2},{4,3},{5,4},{6,5},{7,6},{0,7},{9,8},{10,9},{11,1... | collective-permute-start | bytes 3080 | tf_op jit(solution)/shard_map/ppermute | solution.py:367
  10.7 61.8 %collective-permute-start.5 = (f32[540,1]{1,0:T(8,128)}, f32[540,1]{1,0:T(8,128)S(1)}, u32[]{:S(2)}, u32[]{:S(2)}) collective-permute-start(f32[540,1]{1,0:T(8,128)} %slice.117), channel_id=1, source_target_pairs={{8,0},{16,8},{24,16},{9,1},{17,9},{25,17},{10,2},{18,10},{26,18},{... | collective-permute-start | bytes 6488 | tf_op jit(solution)/shard_map/ppermute | solution.py:368
  13.8 10.3 %copy-start.3 = (f32[540,256]{1,0:T(8,128)}, f32[540,256]{1,0:T(8,128)S(1)}, u32[]{:S(2)}) copy-start(f32[540,256]{1,0:T(8,128)S(1)} %get-tuple-element.16) | copy-start | bytes 1658884
  13.8 10.3 %copy-start.5 = (f32[540,256]{1,0:T(8,128)}, f32[540,256]{1,0:T(8,128)S(1)}, u32[]{:S(2)}) copy-start(f32[540,256]{1,0:T(8,128)S(1)} %get-tuple-element.14) | copy-start | bytes 1658884
  13.8 76.0 %copy-start.2 = (f32[540,256]{1,0:T(8,128)}, f32[540,256]{1,0:T(8,128)S(1)}, u32[]{:S(2)}) copy-start(f32[540,256]{1,0:T(8,128)S(1)} %get-tuple-element.15) | copy-start | bytes 1658884
  14.4 56.7 %collective-permute-start.3 = (f32[1,256]{1,0:T(1,128)}, f32[1,256]{1,0:T(1,128)}, u32[]{:S(2)}, u32[]{:S(2)}) collective-permute-start(f32[1,256]{1,0:T(1,128)} %slice.112), channel_id=1, source_target_pairs={{0,1},{1,2},{2,3},{3,4},{4,5},{5,6},{6,7},{7,0},{8,9},{9,10},{10,1... | collective-permute-start | bytes 3080 | tf_op jit(solution)/shard_map/ppermute | solution.py:369
  15.3 64.1 %collective-permute-start.7 = (f32[540,1]{1,0:T(8,128)}, f32[540,1]{1,0:T(8,128)}, u32[]{:S(2)}, u32[]{:S(2)}) collective-permute-start(f32[540,1]{1,0:T(8,128)} %slice.120), channel_id=1, source_target_pairs={{0,8},{8,16},{16,24},{1,9},{9,17},{17,25},{2,10},{10,18},{18,26},{... | collective-permute-start | bytes 6488 | tf_op jit(solution)/shard_map/ppermute | solution.py:371
  24.7 61.3 %copy-start.4 = (f32[540,256]{1,0:T(8,128)S(1)}, f32[540,256]{1,0:T(8,128)}, u32[]{:S(2)}) copy-start(f32[540,256]{1,0:T(8,128)} %copy-done.3) | copy-start | bytes 1658884
  24.7 61.3 %copy-start.6 = (f32[540,256]{1,0:T(8,128)S(1)}, f32[540,256]{1,0:T(8,128)}, u32[]{:S(2)}) copy-start(f32[540,256]{1,0:T(8,128)} %copy-done.5) | copy-start | bytes 1658884
  24.7 61.3 %copy-start.7 = (f32[539,256]{1,0:T(8,128)S(1)}, f32[539,256]{1,0:T(8,128)}, u32[]{:S(2)}) copy-start(f32[539,256]{1,0:T(8,128)} %slice.108) | copy-start | bytes 1655812
  24.7 61.3 %copy-start.8 = (f32[540,255]{1,0:T(8,128)S(1)}, f32[540,255]{1,0:T(8,128)}, u32[]{:S(2)}) copy-start(f32[540,255]{1,0:T(8,128)} %slice.116) | copy-start | bytes 1652404
  68.8 10.6 %collective-permute-start.2 = (f32[1,256]{1,0:T(1,128)S(1)}, f32[1,256]{1,0:T(1,128)S(1)}, u32[]{:S(2)}, u32[]{:S(2)}) collective-permute-start(f32[1,256]{1,0:T(1,128)S(1)} %get-tuple-element.12), channel_id=1, source_target_pairs={{1,0},{2,1},{3,2},{4,3},{5,4},{6,5},{7,6},{0,7},{9,8},{10,9},{11,1... | collective-permute-start | bytes 3080 | tf_op jit(solution)/shard_map/ppermute | solution.py:380
  71.2 8.2 %collective-permute-start.4 = (f32[1,256]{1,0:T(1,128)S(1)}, f32[1,256]{1,0:T(1,128)S(1)}, u32[]{:S(2)}, u32[]{:S(2)}) collective-permute-start(f32[1,256]{1,0:T(1,128)S(1)} %get-tuple-element.13), channel_id=1, source_target_pairs={{0,1},{1,2},{2,3},{3,4},{4,5},{5,6},{6,7},{7,0},{8,9},{9,10},{10,1... | collective-permute-start | bytes 3080 | tf_op jit(solution)/shard_map/ppermute | solution.py:381
  71.2 13.7 %collective-permute-start.6 = (f32[540,1]{1,0:T(8,128)S(1)}, f32[540,1]{1,0:T(8,128)S(1)}, u32[]{:S(2)}, u32[]{:S(2)}) collective-permute-start(f32[540,1]{1,0:T(8,128)S(1)} %get-tuple-element.19), channel_id=1, source_target_pairs={{8,0},{16,8},{24,16},{9,1},{17,9},{25,17},{10,2},{18,10},{26,18},{... | collective-permute-start | bytes 6488 | tf_op jit(solution)/shard_map/ppermute | solution.py:382
  72.5 13.5 %collective-permute-start.8 = (f32[540,1]{1,0:T(8,128)S(1)}, f32[540,1]{1,0:T(8,128)S(1)}, u32[]{:S(2)}, u32[]{:S(2)}) collective-permute-start(f32[540,1]{1,0:T(8,128)S(1)} %get-tuple-element.20), channel_id=1, source_target_pairs={{0,8},{8,16},{16,24},{1,9},{9,17},{17,25},{2,10},{10,18},{18,26},{... | collective-permute-start | bytes 6488 | tf_op jit(solution)/shard_map/ppermute | solution.py:383
where the time goes:
time: 226 us; the launch traced here: 225 us
  Pallas kernels  86.6 us (38%)
  blocking collectives  82.6 us (37%)
  starting transfers between devices  23.6 us (10%)
  other arithmetic  12.5 us (6%)
  local copies, waits for them, and re-layouts  9.81 us (4%)
  waiting for transfers between devices  6.64 us (3%)
  between operations  3.71 us (2%)
    pallas_call x2, Pallas kernels, precondition(): return call(grown, constants, merid, scale, scale_out)[:length]  86.6 us
    psum x1, blocking collectives, local(): rz_next = lax.psum(jnp.sum(residual * second), ('lat', 'lon'))  42.1 us
    psum x1, blocking collectives, local(): lax.psum(jnp.stack([jnp.sum(rhs_wet * first), jnp.sum(first * image)]), (...  40.5 us
    ppermute x1, starting transfers between devices, local(): from_south = lax.ppermute(first[:, -1:], 'lat', line)  6.8 us
    ppermute x1, waiting for transfers between devices, local(): from_north = lax.ppermute(first[:, :1], 'lat', back_line)  5.41 us
    ppermute x1, starting transfers between devices, local(): lax.ppermute(north_wet[:, -1:], 'lat', line)  5.27 us
    ppermute x1, starting transfers between devices, local(): lax.ppermute(staggered_inverse[count - 1], 'lat', [(i, i + 1) for i in ra...  4.96 us
  transfers between devices with their start and end apart: 9, of which 2 were waited for; matrix products, arithmetic and copies ran while one was open for 5% of the time, Pallas kernels for 19%

commit v1 on v0

--- a/solution.py
+++ b/solution.py
@@ -271,6 +271,77 @@
     @pl.when(go_down)
     def _():
         down.wait_send()
+
+
+def total_kernel(groups, bands, x_ref, out_ref, circle, middle, column, send_sem, recv_sem):
+    band = lax.axis_index("lat")
+    me = lax.axis_index("lon")
+    barrier = pltpu.get_barrier_semaphore()
+    for step in range(1, groups):
+        pl.semaphore_signal(
+            barrier, inc=1, device_id=(band, (me + step) % groups), device_id_type=MESH
+        )
+    for step in range(1, bands):
+        pl.semaphore_signal(
+            barrier, inc=1, device_id=((band + step) % bands, me), device_id_type=MESH
+        )
+    pl.semaphore_wait(barrier, groups + bands - 2)
+
+    def gather(source, target, place, count, first, address):
+        def copy(step, to, slot):
+            return pltpu.make_async_remote_copy(
+                src_ref=source,
+                dst_ref=target.at[slot],
+                send_sem=send_sem.at[first + step],
+                recv_sem=recv_sem.at[first + step],
+                device_id=address(to),
+                device_id_type=MESH,
+            )
+
+        sent = [copy(step, (place + step) % count, place) for step in range(1, count)]
+        for item in sent:
+            item.start()
+        target[place] = source[...]
+        for step in range(1, count):
+            origin = (place - step + count) % count
+            copy(step, origin, origin).wait_recv()
+        total = target[0]
+        for index in range(1, count):
+            total = total + target[index]
+        return total, sent
+
+    total, sent1 = gather(x_ref, circle, me, groups, 0, lambda to: (band, to))
+    middle[...] = total
+    total, sent2 = gather(middle, column, band, bands, groups, lambda to: (to, me))
+    out_ref[...] = total
+    for item in sent1 + sent2:
+        item.wait_send()
+
+
+def totals(values):
+    groups, bands = lax.axis_size("lon"), lax.axis_size("lat")
+    tile = jnp.zeros((8, 128), jnp.float32)
+    row = lax.broadcasted_iota(jnp.int32, (8, 128), 0)
+    for index, value in enumerate(values):
+        tile = jnp.where(row == index, value, tile)
+    vmem = pl.BlockSpec(memory_space=pltpu.VMEM)
+    summed = pl.pallas_call(
+        functools.partial(total_kernel, groups, bands),
+        out_shape=jax.ShapeDtypeStruct((8, 128), jnp.float32),
+        in_specs=[vmem],
+        out_specs=vmem,
+        scratch_shapes=[
+            pltpu.VMEM((groups, 8, 128), jnp.float32),
+            pltpu.VMEM((8, 128), jnp.float32),
+            pltpu.VMEM((bands, 8, 128), jnp.float32),
+            pltpu.SemaphoreType.DMA((groups + bands,)),
+            pltpu.SemaphoreType.DMA((groups + bands,)),
+        ],
+        compiler_params=pltpu.CompilerParams(collective_id=1, has_side_effects=True),
+        cost_estimate=pl.CostEstimate(flops=10_000_000, bytes_accessed=8192, transcendentals=0),
+        name="total",
+    )(tile)
+    return [summed[index, 0] for index in range(len(values))]
 
 
 def local(
@@ -386,16 +457,13 @@
     image = image + west * (first - jnp.concatenate([from_west, first[:-1]], axis=0))
     image = image + north * (first - jnp.concatenate([first[:, 1:], from_north], axis=1))
     image = image + south * (first - jnp.concatenate([from_south, first[:, :-1]], axis=1))
-    sums = lax.psum(
-        jnp.stack([jnp.sum(rhs_wet * first), jnp.sum(first * image)]), ("lat", "lon")
-    )
-    rz_now = sums[0]
-    alpha = rz_now / sums[1]
+    rz_now, curvature = totals([jnp.sum(rhs_wet * first), jnp.sum(first * image)])
+    alpha = rz_now / curvature
     filtered = wet * precondition(image)
     solved = alpha * first
     residual = rhs_wet - alpha * image
     second = first - alpha * filtered
-    rz_next = lax.psum(jnp.sum(residual * second), ("lat", "lon"))
+    (rz_next,) = totals([jnp.sum(residual * second)])
     direction = second + rz_next / rz_now * first
     return (solved, residual, direction)
 

time: 226 us -> 168 us (0.74)
  blocking collectives: 82.6 us -> 0 us
  Pallas kernels: 86.6 us -> 111 us
  local copies, waits for them, and re-layouts: 9.81 us -> 12.7 us
    psum x2 -> x0, blocking collectives: 82.6 us -> none  [the longest x1 42.1 us: local(): rz_next = lax.psum(jnp.sum(residual * second), ('lat', 'lon'))]
    pallas_call x0 -> x2, Pallas kernels: none -> 25.2 us  [totals(): pl.pallas_call(functools.partial(total_kernel, groups, bands), out_shape=...]
    ppermute x1, waiting for transfers between devices: 5.41 us -> 0.01 us  [local(): from_north = lax.ppermute(first[:, :1], 'lat', back_line)]
    select_n x0 -> x3, other arithmetic: none -> 2.61 us  [totals(): tile = jnp.where(row == index, value, tile)]
    ppermute x1, waiting for transfers between devices: 0.01 us -> 2.6 us  [local(): from_west = lax.ppermute(first[-1:], 'lon', ring)]
  transfers between devices with their start and end apart: 9 -> 9, of which waited for: 2 -> 3; matrix products, arithmetic and copies ran while one was open for 5% -> 6% of each run, Pallas kernels for 19% -> 26%
where the time goes in v1:
time: 168 us; the launch traced here: 167 us
  Pallas kernels  111 us (66%)
  starting transfers between devices  22.3 us (13%)
  local copies, waits for them, and re-layouts  12.7 us (8%)
  other arithmetic  12.5 us (7%)
  waiting for transfers between devices  5.02 us (3%)
  between operations  3.75 us (2%)
    pallas_call x2, Pallas kernels, precondition(): return call(grown, constants, merid, scale, scale_out)[:length]  85.5 us
    pallas_call x2, Pallas kernels, totals(): pl.pallas_call(functools.partial(total_kernel, groups, bands), out_shape=...  25.2 us
    ppermute x1, starting transfers between devices, local(): from_south = lax.ppermute(first[:, -1:], 'lat', line)  6.96 us
    ppermute x1, starting transfers between devices, local(): lax.ppermute(staggered_inverse[count - 1], 'lat', [(i, i + 1) for i in ra...  4.96 us
    reduce_sum x1, other arithmetic, local(): jnp.sum(first * image)  3.77 us
    ppermute x1, starting transfers between devices, local(): lax.ppermute(north_wet[:, -1:], 'lat', line)  3.49 us
  transfers between devices with their start and end apart: 9, of which 3 were waited for; matrix products, arithmetic and copies ran while one was open for 6% of the time, Pallas kernels for 26%

profile of v1, /device:TPU:0, one launch (start us, length us, event | category | flops | bytes accessed | tf_op | source)
XLA Modules:
  0.0 167.1 jit_solution(2350217100959940496)
XLA Ops:
  0.6 0.0 copy-start
  0.6 0.0 copy-start.1
  0.7 1.0 fusion.18
  1.7 0.1 copy.18
  1.8 5.0 %collective-permute-start = (f32[128,128]{0,1:T(8,128)S(1)}, f32[128,128]{0,1:T(8,128)S(1)}, u32[]{:S(2)}, u32[]{:S(2)}) collective-permute-start(f32[128,128]{0,1:T(8,128)S(1)} %bitcast.15), channel_id=1, source_target_pairs={{0,8},{8,16},{16,24},{1,9},{9,17},{17,25},{2,10},{10,18},{18,26},{... | collective-permute-start | bytes 196616 | tf_op jit(solution)/shard_map/ppermute | solution.py:380
  6.7 1.7 %convert_multiply_fusion.1 = (f32[540,256]{1,0:T(8,128)S(1)}, f32[540,256]{1,0:T(8,128)S(1)}, f32[540,256]{1,0:T(8,128)S(1)}) fusion(f32[540,256]{1,0:T(8,128)} %param.14, s32[540,256]{1,0:T(8,128)} %param.12, f32[540,256]{1,0:T(8,128)} %param.11, f32[540,256]{1,0:T(8,128)} %param.15), kind=kLoop, calls=%fused_computation.48 | loop fusion | flops 552960 | bytes 3870720 | tf_op jit(solution)/shard_map/mul | solution.py:436
  8.5 0.0 copy-start.5
  8.5 0.0 copy-start.7
  8.5 1.0 slice.124
  9.5 3.5 %collective-permute-start.7 = (f32[540,1]{1,0:T(8,128)}, f32[540,1]{1,0:T(8,128)S(1)}, u32[]{:S(2)}, u32[]{:S(2)}) collective-permute-start(f32[540,1]{1,0:T(8,128)} %slice.124), channel_id=1, source_target_pairs={{0,8},{8,16},{16,24},{1,9},{9,17},{17,25},{2,10},{10,18},{18,26},{... | collective-permute-start | bytes 6488 | tf_op jit(solution)/shard_map/ppermute | solution.py:442
  13.0 0.6 slice.116
  13.6 0.0 collective-permute-start.3
  13.6 1.1 convert_element_type.6
  14.7 0.7 slice.121
  15.5 1.3 collective-permute-start.5
  16.8 0.5 slice.113
  17.3 2.6 %collective-permute-start.1 = (f32[1,256]{1,0:T(1,128)}, f32[1,256]{1,0:T(1,128)}, u32[]{:S(2)}, u32[]{:S(2)}) collective-permute-start(f32[1,256]{1,0:T(1,128)} %slice.113), channel_id=1, source_target_pairs={{1,0},{2,1},{3,2},{4,3},{5,4},{6,5},{7,6},{0,7},{9,8},{10,9},{11,1... | collective-permute-start | bytes 3080 | tf_op jit(solution)/shard_map/ppermute | solution.py:438
  20.0 0.8 slice.112
  20.8 1.0 slice.120
  21.8 0.1 copy.19
  21.9 0.1 copy.17
  22.1 0.1 copy.14
  22.2 0.8 dynamic_slice.20
  23.0 0.9 dynamic-slice_reduce_fusion
  23.9 0.0 copy-start.8
  23.9 0.4 broadcast_multiply_fusion
  24.3 0.0 collective-permute-done
  24.3 0.1 fusion.19
  24.4 0.1 fusion.12
  24.5 0.1 fusion.9.merid_ref
  24.6 43.2 %zonal_precondition.2 = f32[576,256]{1,0:T(8,128)S(1)} custom-call(f32[576,256]{1,0:T(8,128)S(1)} %pad.11.x_ref, bf16[4,2,1152,1152]{3,2,1,0:T(8,128)(2,1)} %constant.64.clone.matrix_ref, f32[256,128]{1,0:T(8,128)S(1)} %fusion.9.merid_ref, f32[1152,128]{1,0:T(8,128)S(1)} %get-tuple-element.29.scale_ref, f32[1152,128]{1,0:T(8,128)S(1)} %get-tuple-element.28.scale_out_ref), custom_call_target="tpu_custom_call" | custom-call | flops 5898240000 | bytes 10616832 | tf_op jit(solution)/shard_map/zonal_precondition/pallas_call | solution.py:428
  67.7 0.0 copy-done.1
  67.8 0.1 slice_multiply_fusion
  67.8 0.1 fusion.14
  67.9 0.1 fusion.17
  68.1 1.3 collective-permute-start.6
  69.4 0.0 collective-permute-done.3
  69.4 7.0 %collective-permute-start.8 = (f32[540,1]{1,0:T(8,128)S(1)}, f32[540,1]{1,0:T(8,128)S(1)}, u32[]{:S(2)}, u32[]{:S(2)}) collective-permute-start(f32[540,1]{1,0:T(8,128)S(1)} %get-tuple-element.20), channel_id=1, source_target_pairs={{0,8},{8,16},{16,24},{1,9},{9,17},{17,25},{2,10},{10,18},{18,26},{... | collective-permute-start | bytes 6488 | tf_op jit(solution)/shard_map/ppermute | solution.py:454
  76.3 0.0 collective-permute-done.1
  76.4 1.7 %collective-permute-start.2 = (f32[1,256]{1,0:T(1,128)S(1)}, f32[1,256]{1,0:T(1,128)S(1)}, u32[]{:S(2)}, u32[]{:S(2)}) collective-permute-start(f32[1,256]{1,0:T(1,128)S(1)} %get-tuple-element.12), channel_id=1, source_target_pairs={{1,0},{2,1},{3,2},{4,3},{5,4},{6,5},{7,6},{0,7},{9,8},{10,9},{11,1... | collective-permute-start | bytes 3080 | tf_op jit(solution)/shard_map/ppermute | solution.py:451
  78.0 0.0 collective-permute-done.7
  78.0 0.0 collective-permute-start.4
  78.0 0.2 fusion.16
  78.3 0.0 collective-permute-done.5
  78.3 1.1 collective-permute-done.2
  79.3 2.6 %collective-permute-done.4 = f32[1,256]{1,0:T(1,128)S(1)} collective-permute-done((f32[1,256]{1,0:T(1,128)S(1)}, f32[1,256]{1,0:T(1,128)S(1)}, u32[]{:S(2)}, u32[]{:S(2)}) %collective-permute-start.4) | collective-permute-done | bytes 1056 | tf_op jit(solution)/shard_map/ppermute | solution.py:452
  81.9 0.0 collective-permute-done.6
  81.9 1.3 collective-permute-done.8
  83.3 0.0 copy-done.6
  83.3 3.8 %multiply_reduce_fusion.2 = (f32[]{:T(128)}, f32[]{:T(128)}, f32[540,256]{1,0:T(8,128)}) fusion(f32[540,256]{1,0:T(8,128)S(1)} %slice_multiply_fusion, f32[540,256]{1,0:T(8,128)S(1)} %get-tuple-element.15, f32[540,255]{1,0:T(8,128)S(1)} %get-tuple-element.18, f32[540,1]{1,0:T(8,128)S(1)} %collective-permute-done.8, f32[540,255]{1,0:T(8,128)S(1)} %bitcast.12, ...), kind=kLoop, calls=%fused_computation.22 | loop fusion | flops 4838398 | bytes 8294408 | tf_op jit(solution)/shard_map/reduce_sum | solution.py:460
  87.1 0.0 copy-done.2
  87.1 0.6 compare_select_fusion.1
  87.7 1.3 broadcast_select_fusion.x_ref
  89.0 12.4 %total.2 = f32[8,128]{1,0:T(8,128)} custom-call(f32[8,128]{1,0:T(8,128)} %broadcast_select_fusion.x_ref), custom_call_target="tpu_custom_call" | custom-call | flops 10000000 | bytes 8192 | tf_op jit(solution)/shard_map/total/pallas_call | solution.py:328
  101.4 0.0 copy-start.4
  101.4 1.4 fusion.21
  102.8 1.1 pad.12.x_ref
  103.9 42.4 %zonal_precondition.3 = f32[576,256]{1,0:T(8,128)S(1)} custom-call(f32[576,256]{1,0:T(8,128)S(1)} %pad.12.x_ref, bf16[4,2,1152,1152]{3,2,1,0:T(8,128)(2,1)} %constant.64.clone.matrix_ref, f32[256,128]{1,0:T(8,128)S(1)} %fusion.9.merid_ref, f32[1152,128]{1,0:T(8,128)S(1)} %get-tuple-element.29.scale_ref, f32[1152,128]{1,0:T(8,128)S(1)} %get-tuple-element.28.scale_out_ref), custom_call_target="tpu_custom_call" | custom-call | flops 5898240000 | bytes 10616832 | tf_op jit(solution)/shard_map/zonal_precondition/pallas_call | solution.py:428
  147.7 1.6 multiply_reduce_fusion
  149.2 0.6 compare_select_fusion
  149.9 0.7 iota.20.x_ref
  150.5 12.9 %total.3 = f32[8,128]{1,0:T(8,128)} custom-call(f32[8,128]{1,0:T(8,128)} %iota.20.x_ref), custom_call_target="tpu_custom_call" | custom-call | flops 10000000 | bytes 8192 | tf_op jit(solution)/shard_map/total/pallas_call | solution.py:328
  163.4 1.2 slice.107
  166.0 1.1 multiply_add_fusion
  (19 shorter events, 0.1 us)
Async XLA Ops:
  0.6 21.4 %copy-start = (f32[2,128,128]{2,1,0:T(8,128)S(1)}, f32[2,128,128]{2,1,0:T(8,128)}, u32[]{:S(2)}) copy-start(f32[2,128,128]{2,1,0:T(8,128)} %param.17) | copy-start | bytes 393220
  0.6 67.1 %copy-start.1 = (s32[540,256]{1,0:T(8,128)S(1)}, s32[540,256]{1,0:T(8,128)}, u32[]{:S(2)}) copy-start(s32[540,256]{1,0:T(8,128)} %param.12) | copy-start | bytes 1658884
  1.8 22.5 %collective-permute-start = (f32[128,128]{0,1:T(8,128)S(1)}, f32[128,128]{0,1:T(8,128)S(1)}, u32[]{:S(2)}, u32[]{:S(2)}) collective-permute-start(f32[128,128]{0,1:T(8,128)S(1)} %bitcast.15), channel_id=1, source_target_pairs={{0,8},{8,16},{16,24},{1,9},{9,17},{17,25},{2,10},{10,18},{18,26},{... | collective-permute-start | bytes 196616 | tf_op jit(solution)/shard_map/ppermute | solution.py:380
  8.5 5.2 %copy-start.5 = (f32[540,256]{1,0:T(8,128)}, f32[540,256]{1,0:T(8,128)S(1)}, u32[]{:S(2)}) copy-start(f32[540,256]{1,0:T(8,128)S(1)} %get-tuple-element.16) | copy-start | bytes 1658884
  8.5 15.4 %copy-start.7 = (f32[540,256]{1,0:T(8,128)}, f32[540,256]{1,0:T(8,128)S(1)}, u32[]{:S(2)}) copy-start(f32[540,256]{1,0:T(8,128)S(1)} %get-tuple-element.14) | copy-start | bytes 1658884
  8.5 78.6 %copy-start.2 = (f32[540,256]{1,0:T(8,128)}, f32[540,256]{1,0:T(8,128)S(1)}, u32[]{:S(2)}) copy-start(f32[540,256]{1,0:T(8,128)S(1)} %get-tuple-element.15) | copy-start | bytes 1658884
  9.5 68.5 %collective-permute-start.7 = (f32[540,1]{1,0:T(8,128)}, f32[540,1]{1,0:T(8,128)S(1)}, u32[]{:S(2)}, u32[]{:S(2)}) collective-permute-start(f32[540,1]{1,0:T(8,128)} %slice.124), channel_id=1, source_target_pairs={{0,8},{8,16},{16,24},{1,9},{9,17},{17,25},{2,10},{10,18},{18,26},{... | collective-permute-start | bytes 6488 | tf_op jit(solution)/shard_map/ppermute | solution.py:442
  13.6 55.7 %collective-permute-start.3 = (f32[1,256]{1,0:T(1,128)}, f32[1,256]{1,0:T(1,128)}, u32[]{:S(2)}, u32[]{:S(2)}) collective-permute-start(f32[1,256]{1,0:T(1,128)} %slice.116), channel_id=1, source_target_pairs={{0,1},{1,2},{2,3},{3,4},{4,5},{5,6},{6,7},{7,0},{8,9},{9,10},{10,1... | collective-permute-start | bytes 3080 | tf_op jit(solution)/shard_map/ppermute | solution.py:440
  15.5 62.8 %collective-permute-start.5 = (f32[540,1]{1,0:T(8,128)}, f32[540,1]{1,0:T(8,128)}, u32[]{:S(2)}, u32[]{:S(2)}) collective-permute-start(f32[540,1]{1,0:T(8,128)} %slice.121), channel_id=1, source_target_pairs={{8,0},{16,8},{24,16},{9,1},{17,9},{25,17},{10,2},{18,10},{26,18},{... | collective-permute-start | bytes 6488 | tf_op jit(solution)/shard_map/ppermute | solution.py:439
  17.3 59.0 %collective-permute-start.1 = (f32[1,256]{1,0:T(1,128)}, f32[1,256]{1,0:T(1,128)}, u32[]{:S(2)}, u32[]{:S(2)}) collective-permute-start(f32[1,256]{1,0:T(1,128)} %slice.113), channel_id=1, source_target_pairs={{1,0},{2,1},{3,2},{4,3},{5,4},{6,5},{7,6},{0,7},{9,8},{10,9},{11,1... | collective-permute-start | bytes 3080 | tf_op jit(solution)/shard_map/ppermute | solution.py:438
  22.9 60.3 %copy-start.6 = (f32[540,256]{1,0:T(8,128)S(1)}, f32[540,256]{1,0:T(8,128)}, u32[]{:S(2)}) copy-start(f32[540,256]{1,0:T(8,128)} %copy-done.5) | copy-start | bytes 1658884
  22.9 60.3 %copy-start.9 = (f32[539,256]{1,0:T(8,128)S(1)}, f32[539,256]{1,0:T(8,128)}, u32[]{:S(2)}) copy-start(f32[539,256]{1,0:T(8,128)} %slice.112) | copy-start | bytes 1655812
  22.9 60.3 %copy-start.10 = (f32[540,255]{1,0:T(8,128)S(1)}, f32[540,255]{1,0:T(8,128)}, u32[]{:S(2)}) copy-start(f32[540,255]{1,0:T(8,128)} %slice.120) | copy-start | bytes 1652404
  23.9 59.4 %copy-start.8 = (f32[540,256]{1,0:T(8,128)S(1)}, f32[540,256]{1,0:T(8,128)}, u32[]{:S(2)}) copy-start(f32[540,256]{1,0:T(8,128)} %copy-done.7) | copy-start | bytes 1658884
  68.1 13.9 %collective-permute-start.6 = (f32[540,1]{1,0:T(8,128)S(1)}, f32[540,1]{1,0:T(8,128)S(1)}, u32[]{:S(2)}, u32[]{:S(2)}) collective-permute-start(f32[540,1]{1,0:T(8,128)S(1)} %get-tuple-element.19), channel_id=1, source_target_pairs={{8,0},{16,8},{24,16},{9,1},{17,9},{25,17},{10,2},{18,10},{26,18},{... | collective-permute-start | bytes 6488 | tf_op jit(solution)/shard_map/ppermute | solution.py:453
  69.4 13.9 %collective-permute-start.8 = (f32[540,1]{1,0:T(8,128)S(1)}, f32[540,1]{1,0:T(8,128)S(1)}, u32[]{:S(2)}, u32[]{:S(2)}) collective-permute-start(f32[540,1]{1,0:T(8,128)S(1)} %get-tuple-element.20), channel_id=1, source_target_pairs={{0,8},{8,16},{16,24},{1,9},{9,17},{17,25},{2,10},{10,18},{18,26},{... | collective-permute-start | bytes 6488 | tf_op jit(solution)/shard_map/ppermute | solution.py:454
  76.4 3.0 %collective-permute-start.2 = (f32[1,256]{1,0:T(1,128)S(1)}, f32[1,256]{1,0:T(1,128)S(1)}, u32[]{:S(2)}, u32[]{:S(2)}) collective-permute-start(f32[1,256]{1,0:T(1,128)S(1)} %get-tuple-element.12), channel_id=1, source_target_pairs={{1,0},{2,1},{3,2},{4,3},{5,4},{6,5},{7,6},{0,7},{9,8},{10,9},{11,1... | collective-permute-start | bytes 3080 | tf_op jit(solution)/shard_map/ppermute | solution.py:451
  78.0 3.9 %collective-permute-start.4 = (f32[1,256]{1,0:T(1,128)S(1)}, f32[1,256]{1,0:T(1,128)S(1)}, u32[]{:S(2)}, u32[]{:S(2)}) collective-permute-start(f32[1,256]{1,0:T(1,128)S(1)} %get-tuple-element.13), channel_id=1, source_target_pairs={{0,1},{1,2},{2,3},{3,4},{4,5},{5,6},{6,7},{7,0},{8,9},{9,10},{10,1... | collective-permute-start | bytes 3080 | tf_op jit(solution)/shard_map/ppermute | solution.py:452
  101.4 46.2 %copy-start.3 = (f32[540,256]{1,0:T(8,128)S(1)}, f32[540,256]{1,0:T(8,128)}, u32[]{:S(2)}) copy-start(f32[540,256]{1,0:T(8,128)} %copy-done.2) | copy-start | bytes 1658884
  101.4 46.2 %copy-start.4 = (f32[540,256]{1,0:T(8,128)S(1)}, f32[540,256]{1,0:T(8,128)}, u32[]{:S(2)}) copy-start(f32[540,256]{1,0:T(8,128)} %get-tuple-element.7) | copy-start | bytes 1658884
